TPU v7x, 32 devices: a whole 2x2x4 slice. The times are simulated.
32 devices in a mesh: row: 4 (over y, x), col: 8 (over z, core).
Axes of the slice: x: 2, y: 2, z: 4, core: 2. Of those that a mesh axis runs over, the one named last changes fastest.
Arguments:
- points: bfloat16 [10240, 64], P(('row', 'col')), may hold values from -5 to 5
- start_vectors: bfloat16 [10240, 32], P(('row', 'col')), may hold values from -12 to 12
Outputs:
- basis: float32 [10240, 32], P(('row', 'col'))
All inputs are finite; a program needn't handle non-finite values.
Results may differ from a plain program's by a relative error of at most 0.007.
Values may be sent and summed in bfloat16 or wider, within the bound.
A program may use at most 64 MiB of HBM per device.

v0:
```python
import jax
import jax.numpy as jnp
from jax import lax
from jax.sharding import PartitionSpec as P

ITERS = 2
KERNEL_SCALE = 5.12


def squared_norms(values):
    return jnp.sum(jnp.square(values.astype(jnp.float32)), axis=1)


def affinity(block_pts, block_sq, col_pts, col_sq):
    features = block_pts.shape[1]
    cross = lax.dot_general(
        block_pts, col_pts, (((1,), (1,)), ((), ())), preferred_element_type=jnp.float32
    )
    dist = block_sq[:, None] + col_sq[None, :] - 2.0 * cross
    return jnp.exp(dist * (-KERNEL_SCALE / features)).astype(jnp.bfloat16)


def sweep(row_pts, row_sq, col_pts, col_sq, panel, with_degree):
    rows, features = row_pts.shape
    height = min(512, rows)
    count = rows // height
    stacked = (row_pts.reshape(count, height, features), row_sq.reshape(count, height))

    def one_block(item):
        weights = affinity(item[0], item[1], col_pts, col_sq)
        results = ()
        if panel is not None:
            results = results + (jnp.dot(weights, panel, preferred_element_type=jnp.float32),)
        if with_degree:
            results = results + (jnp.sum(weights, axis=1, dtype=jnp.float32),)
        return results

    mapped = lax.map(one_block, stacked)
    return [piece.reshape((rows,) + piece.shape[2:]) for piece in mapped]


def orthonormal(product, degree, total):
    scaled = product / degree[:, None]
    gram_part = jnp.dot(
        scaled.T, scaled, precision=lax.Precision.HIGHEST, preferred_element_type=jnp.float32
    )
    gram = lax.psum(gram_part, ("row", "col"))
    lower = jnp.linalg.cholesky(gram / total)
    return lax.linalg.triangular_solve(lower, scaled, left_side=False, lower=True, transpose_a=True)


def shards(points, start_vectors):
    group = points.shape[0]
    total = group * lax.axis_size("row") * lax.axis_size("col")
    row_pts = lax.all_gather(points, "col", axis=0, tiled=True)
    col_pts = lax.all_gather(points, "row", axis=0, tiled=True)
    row_sq = squared_norms(row_pts)
    col_sq = squared_norms(col_pts)
    degree_part = sweep(row_pts, row_sq, col_pts, col_sq, None, True)[0]
    vectors = start_vectors
    ortho = jnp.zeros(start_vectors.shape, jnp.float32)
    degree = None
    for step in range(ITERS):
        panel = lax.all_gather(vectors, "row", axis=0, tiled=True)
        if step == 0:
            product_part = sweep(row_pts, row_sq, col_pts, col_sq, panel, False)[0]
            product, degree = (
                lax.psum_scatter(product_part, "col", scatter_dimension=0, tiled=True),
                lax.psum_scatter(degree_part, "col", scatter_dimension=0, tiled=True),
            )
        else:
            product_part = sweep(row_pts, row_sq, col_pts, col_sq, panel, False)[0]
            product = lax.psum_scatter(product_part, "col", scatter_dimension=0, tiled=True)
        ortho = orthonormal(product, degree, total)
        vectors = ortho.astype(jnp.bfloat16)
    return ortho


def solution(mesh):
    return jax.shard_map(
        shards,
        mesh=mesh,
        in_specs=(P(("row", "col"), None), P(("row", "col"), None)),
        out_specs=P(("row", "col"), None),
        check_vma=False,
    )
```

profile of v0, /device:TPU:10, one launch (start us, length us, event | category | flops | bytes accessed | tf_op | source)
XLA Modules:
  0.0 230.9 jit_solution(14613255640322226920)
XLA Ops:
  6.5 14.9 %all-gather = bf16[8,320,64]{1,2,0:T(8,128)(2,1)S(1)} all-gather(bf16[1,320,64]{1,2,0:T(8,128)(2,1)} %bitcast.101), channel_id=1, replica_groups=mesh['row'=4,'col'=8] {'col'}, dimensions={0}, use_global_device_ids=true | all-gather | bytes 368640 | tf_op jit(solution)/shard_map/all_gather | solution.py:55
  21.5 8.7 %all-gather.1 = bf16[4,320,64]{1,2,0:T(8,128)(2,1)S(1)} all-gather(bf16[1,320,64]{1,2,0:T(8,128)(2,1)} %bitcast.102), channel_id=1, replica_groups=mesh['row'=4,'col'=8] {'row'}, dimensions={0}, use_global_device_ids=true | all-gather | bytes 204800 | tf_op jit(solution)/shard_map/all_gather | solution.py:56
  30.5 0.2 copy.42
  30.8 0.3 copy.55
  31.3 7.6 %all-gather.2 = bf16[4,320,32]{1,2,0:T(8,128)(2,1)S(1)} all-gather(bf16[1,320,32]{1,2,0:T(8,128)(2,1)S(1)} %bitcast.107), channel_id=1, replica_groups=mesh['row'=4,'col'=8] {'row'}, dimensions={0}, use_global_device_ids=true | all-gather | bytes 102400 | tf_op jit(solution)/shard_map/all_gather | solution.py:64
  38.9 0.2 copy.49
  39.2 4.9 %while.30 = (s32[]{:T(128)}, f32[5,512,32]{1,2,0:T(8,128)S(1)}, f32[5,512]{1,0:T(8,128)S(1)}, f32[1280]{0:T(1024)S(1)}, bf16[5,512,64]{2,1,0:T(8,128)(2,1)S(1)},...) while((s32[]{:T(128)}, f32[5,512,32]{1,2,0:T(8,128)S(1)}, ...), condition=%wide.region_3.4_spmd, body=%wide.region_2.3_spmd.sunk | while | flops 129105920 | bytes 867417 | solution.py:38
  39.2 1.0 fusion.78
  40.2 1.0 fusion.78
  41.2 1.0 fusion.78
  42.2 1.0 fusion.78
  43.1 1.0 fusion.78
  44.1 1.5 copy.58
  45.7 4.8 %while.31 = (s32[]{:T(128)}, f32[5,512]{1,0:T(8,128)S(1)}, f32[5,512]{1,0:T(8,128)S(1)}, f32[1280]{0:T(1024)S(1)}, bf16[5,512,64]{2,1,0:T(8,128)(2,1)S(1)}, /*in...) while((s32[]{:T(128)}, f32[5,512]{1,0:T(8,128)S(1)}, f32[5,512]{1,0:T(8,128)S(1)}, f32[1280]{0:T(1024)S(1)}, ...), condition=%wide.region_7.8_spmd, body=%wide.region_5.7_spmd.sunk | while | flops 88473088 | bytes 479329 | solution.py:38
  45.7 0.9 fusion.81
  46.7 0.9 fusion.81
  47.6 0.9 fusion.81
  48.6 0.9 fusion.81
  49.5 0.9 fusion.81
  50.5 0.6 dynamic-slice
  51.7 22.6 %all-reduce = f32[2560]{0:T(1024)S(1)} all-reduce(f32[2560]{0:T(1024)S(1)} %reshape.43), channel_id=3, replica_groups=mesh['row'=4,'col'=8] {'col'}, use_global_device_ids=true, to_apply=%region_8.9.clone | all-reduce | flops 2560 | bytes 20480
  74.4 1.8 reduce-scatter.7.cloned.1.call-done
  76.2 1.0 copy.52
  77.2 0.2 fusion.49
  77.5 43.7 %psum.14 = f32[32,32]{0,1:T(8,128)S(1)} all-reduce(f32[32,32]{0,1:T(8,128)S(1)} %fusion.49), channel_id=1, replica_groups=mesh['row'=4,'col'=8] {'row','col'}, use_global_device_ids=true, to_apply=%region_9.10 | all-reduce | flops 1024 | bytes 8192 | tf_op jit(solution)/shard_map/psum | solution.py:47
  121.2 2.9 %cholesky.44 = f32[32,32]{1,0:T(8,128)S(1)} custom-call(f32[32,32]{1,0:T(8,128)S(1)} %fusion.56), custom_call_target="Cholesky" | custom-call | tf_op jit(solution)/shard_map/jit(cholesky)/cholesky | solution.py:48
  124.2 0.7 compare_reduce_fusion.1
  124.9 0.7 fusion.51
  125.6 2.4 %custom-call.6 = f32[1,32,32]{1,2,0:T(8,128)S(1)} custom-call(f32[1,32,32]{2,1,0:T(8,128)S(1)} %fusion.51), custom_call_target="InvertDiagBlocksLowerTriangular" | custom-call | tf_op jit(solution)/shard_map/triangular_solve/custom-call.0 | solution.py:49
  128.0 0.3 fusion.48
  128.3 7.6 %all-gather.3 = bf16[4,320,32]{1,2,0:T(8,128)(2,1)S(1)} all-gather(bf16[1,320,32]{1,2,0:T(8,128)(2,1)S(1)} %fusion.48), channel_id=1, replica_groups=mesh['row'=4,'col'=8] {'row'}, dimensions={0}, use_global_device_ids=true | all-gather | bytes 102400 | tf_op jit(solution)/shard_map/all_gather | solution.py:64
  135.9 0.2 copy.50
  136.1 4.9 %while.32 = (s32[]{:T(128)}, f32[5,512,32]{1,2,0:T(8,128)S(1)}, f32[5,512]{1,0:T(8,128)S(1)}, f32[1280]{0:T(1024)S(1)}, bf16[5,512,64]{2,1,0:T(8,128)(2,1)S(1)},...) while((s32[]{:T(128)}, f32[5,512,32]{1,2,0:T(8,128)S(1)}, ...), condition=%wide.region_13.16_spmd, body=%wide.region_12.15_spmd.sunk | while | flops 129105920 | bytes 867417 | solution.py:38
  136.2 1.0 fusion.85
  137.1 1.0 fusion.85
  138.1 1.0 fusion.85
  139.1 1.0 fusion.85
  140.1 1.0 fusion.85
  141.0 1.5 copy.60
  142.5 28.8 %reduce-scatter.9.cloned.1.call-done = f32[320,32]{1,0:T(8,128)} async-done(((f32[2560,32]{1,0:T(8,128)}), f32[320,32]{1,0:T(8,128)}) %reduce-scatter.9.cloned.1.call-update) | async-done | bytes 40976
  171.3 1.0 copy.54
  172.3 0.2 fusion.50
  172.6 43.8 %psum.15 = f32[32,32]{0,1:T(8,128)S(1)} all-reduce(f32[32,32]{0,1:T(8,128)S(1)} %fusion.50), channel_id=1, replica_groups=mesh['row'=4,'col'=8] {'row','col'}, use_global_device_ids=true, to_apply=%region_15.18 | all-reduce | flops 1024 | bytes 8192 | tf_op jit(solution)/shard_map/psum | solution.py:47
  216.5 2.9 %cholesky.55 = f32[32,32]{1,0:T(8,128)S(1)} custom-call(f32[32,32]{1,0:T(8,128)S(1)} %fusion.54), custom_call_target="Cholesky" | custom-call | tf_op jit(solution)/shard_map/jit(cholesky)/cholesky | solution.py:48
  219.4 0.6 compare_reduce_fusion
  220.1 0.7 fusion.52
  220.7 2.4 %custom-call.7 = f32[1,32,32]{1,2,0:T(8,128)S(1)} custom-call(f32[1,32,32]{2,1,0:T(8,128)S(1)} %fusion.52), custom_call_target="InvertDiagBlocksLowerTriangular" | custom-call | tf_op jit(solution)/shard_map/triangular_solve/custom-call.0 | solution.py:49
  223.1 0.9 convolution_bitcast_fusion
  (46 shorter events, 1.4 us)
Async XLA Ops:
  6.5 69.7 %reduce-scatter.7.cloned.1.call-start = ((), (), s32[]{:S(2)}) async-start(), calls=%async_computation.2 | async-start | bytes 1474560
  30.3 1.0 copy-start
  45.6 125.7 %reduce-scatter.9.cloned.1.call-start = ((), (), s32[]{:S(2)}) async-start(), calls=%async_computation.3 | async-start | bytes 1474560
  45.7 4.8 %copy-start.1 = (u32[32]{0:T(128)S(1)}, u32[32]{0:T(128)}, u32[]{:S(2)}) copy-start(u32[32]{0:T(128)} %constant.83) | copy-start | bytes 388
Sparse Core Ops, SparseCore 0:
  45.7 30.4 reduce-scatter.6
  142.7 28.6 reduce-scatter.8
where the time goes:
time: 231 us
  blocking collectives  149 us (65%)
  waiting for transfers between devices  30.6 us (13%)
  matrix products  15.5 us (7%)
  between operations  14.2 us (6%)
  other arithmetic  13.7 us (6%)
  local copies, waits for them, and re-layouts  7.7 us (3%)
    psum x2, blocking collectives, orthonormal(): gram = lax.psum(gram_part, ('row', 'col'))  87.5 us
    unnamed x4, waiting for transfers between devices  30.6 us
    unnamed x1, blocking collectives  22.6 us
    all_gather x2, blocking collectives, shards(): panel = lax.all_gather(vectors, 'row', axis=0, tiled=True)  15.2 us
    all_gather x1, blocking collectives, shards(): row_pts = lax.all_gather(points, 'col', axis=0, tiled=True)  14.9 us
    dot_general x10, matrix products, one_block(): jnp.dot(weights, panel, preferred_element_type=jnp.float32)  9.58 us
    all_gather x1, blocking collectives, shards(): col_pts = lax.all_gather(points, 'row', axis=0, tiled=True)  8.71 us
    another operation x6, other arithmetic, orthonormal(): lower = jnp.linalg.cholesky(gram / total)  7.27 us
  transfers between devices with their start and end apart: 2, of which 2 were waited for; matrix products, arithmetic and copies ran while one was open for 2% of the time, Pallas kernels for 0%

commit v1 on v0

--- a/solution.py
+++ b/solution.py
@@ -44,7 +44,7 @@
     gram_part = jnp.dot(
         scaled.T, scaled, precision=lax.Precision.HIGHEST, preferred_element_type=jnp.float32
     )
-    gram = lax.psum(gram_part, ("row", "col"))
+    gram = jnp.sum(lax.all_gather(gram_part, ("row", "col")), axis=0)
     lower = jnp.linalg.cholesky(gram / total)
     return lax.linalg.triangular_solve(lower, scaled, left_side=False, lower=True, transpose_a=True)
 

time: 231 us -> 232 us (level)
  the two profiles are of different devices: /device:TPU:10 before, /device:TPU:0 now
where the time goes in v1:
time: 232 us; the launch traced here: 231 us
  blocking collectives  147 us (63%)
  waiting for transfers between devices  33.1 us (14%)
  matrix products  15.5 us (7%)
  between operations  14.2 us (6%)
  other arithmetic  13.8 us (6%)
  local copies, waits for them, and re-layouts  7.83 us (3%)
    all_gather x2, blocking collectives, orthonormal(): gram = jnp.sum(lax.all_gather(gram_part, ('row', 'col')), axis=0)  79.9 us
    unnamed x4, waiting for transfers between devices  33.1 us
    unnamed x1, blocking collectives  25.9 us
    all_gather x1, blocking collectives, shards(): row_pts = lax.all_gather(points, 'col', axis=0, tiled=True)  16.4 us
    all_gather x2, blocking collectives, shards(): panel = lax.all_gather(vectors, 'row', axis=0, tiled=True)  15.5 us
    dot_general x10, matrix products, one_block(): jnp.dot(weights, panel, preferred_element_type=jnp.float32)  9.6 us
    all_gather x1, blocking collectives, shards(): col_pts = lax.all_gather(points, 'row', axis=0, tiled=True)  8.96 us
    another operation x6, other arithmetic, orthonormal(): lower = jnp.linalg.cholesky(gram / total)  7.27 us
  transfers between devices with their start and end apart: 2, of which 2 were waited for; matrix products, arithmetic and copies ran while one was open for 2% of the time, Pallas kernels for 0%

profile of v1, /device:TPU:0, one launch (start us, length us, event | category | flops | bytes accessed | tf_op | source)
XLA Modules:
  0.0 231.4 jit_solution(12904690851949806799)
XLA Ops:
  6.5 16.4 %all-gather.2 = bf16[8,320,64]{1,2,0:T(8,128)(2,1)S(1)} all-gather(bf16[1,320,64]{1,2,0:T(8,128)(2,1)} %bitcast.105), channel_id=1, replica_groups=mesh['row'=4,'col'=8] {'col'}, dimensions={0}, use_global_device_ids=true | all-gather | bytes 368640 | tf_op jit(solution)/shard_map/all_gather | solution.py:55
  23.0 9.0 %all-gather.3 = bf16[4,320,64]{1,2,0:T(8,128)(2,1)S(1)} all-gather(bf16[1,320,64]{1,2,0:T(8,128)(2,1)} %bitcast.106), channel_id=1, replica_groups=mesh['row'=4,'col'=8] {'row'}, dimensions={0}, use_global_device_ids=true | all-gather | bytes 204800 | tf_op jit(solution)/shard_map/all_gather | solution.py:56
  32.3 0.2 copy.38
  32.5 0.3 copy.49
  33.1 8.1 %all-gather.4 = bf16[4,320,32]{1,2,0:T(8,128)(2,1)S(1)} all-gather(bf16[1,320,32]{1,2,0:T(8,128)(2,1)S(1)} %bitcast.111), channel_id=1, replica_groups=mesh['row'=4,'col'=8] {'row'}, dimensions={0}, use_global_device_ids=true | all-gather | bytes 102400 | tf_op jit(solution)/shard_map/all_gather | solution.py:64
  41.1 0.2 copy.43
  41.4 4.9 %while.30 = (s32[]{:T(128)}, f32[5,512,32]{1,2,0:T(8,128)S(1)}, f32[5,512]{1,0:T(8,128)S(1)}, f32[1280]{0:T(1024)S(1)}, bf16[5,512,64]{2,1,0:T(8,128)(2,1)S(1)},...) while((s32[]{:T(128)}, f32[5,512,32]{1,2,0:T(8,128)S(1)}, ...), condition=%wide.region_3.4_spmd, body=%wide.region_2.3_spmd.sunk | while | flops 129105920 | bytes 867417 | solution.py:38
  41.4 1.0 fusion.78
  42.4 1.0 fusion.78
  43.4 1.0 fusion.78
  44.4 1.0 fusion.78
  45.4 1.0 fusion.78
  46.3 1.5 copy.52
  47.9 4.8 %while.31 = (s32[]{:T(128)}, f32[5,512]{1,0:T(8,128)S(1)}, f32[5,512]{1,0:T(8,128)S(1)}, f32[1280]{0:T(1024)S(1)}, bf16[5,512,64]{2,1,0:T(8,128)(2,1)S(1)}, /*in...) while((s32[]{:T(128)}, f32[5,512]{1,0:T(8,128)S(1)}, f32[5,512]{1,0:T(8,128)S(1)}, f32[1280]{0:T(1024)S(1)}, ...), condition=%wide.region_7.8_spmd, body=%wide.region_5.7_spmd.sunk | while | flops 88473088 | bytes 479329 | solution.py:38
  47.9 0.9 fusion.81
  48.9 0.9 fusion.81
  49.8 0.9 fusion.81
  50.8 0.9 fusion.81
  51.7 0.9 fusion.81
  52.7 0.6 dynamic-slice
  53.9 25.9 %all-reduce = f32[2560]{0:T(1024)S(1)} all-reduce(f32[2560]{0:T(1024)S(1)} %reshape.43), channel_id=5, replica_groups=mesh['row'=4,'col'=8] {'col'}, use_global_device_ids=true, to_apply=%region_8.9.clone | all-reduce | flops 2560 | bytes 20480
  79.9 1.5 reduce-scatter.7.cloned.1.call-done
  81.5 1.0 copy.46
  82.5 0.2 fusion.49
  82.7 39.9 %all-gather = f32[1024,32]{1,0:T(8,128)S(1)} all-gather(f32[32,32]{1,0:T(8,128)S(1)} %fusion.49), channel_id=2, replica_groups=mesh['row'=4,'col'=8] {'row','col'}, dimensions={0}, use_global_device_ids=true | all-gather | bytes 135168 | tf_op jit(solution)/shard_map/all_gather | solution.py:47
  122.9 2.9 %cholesky.44 = f32[32,32]{1,0:T(8,128)S(1)} custom-call(f32[32,32]{1,0:T(8,128)S(1)} %fusion.56), custom_call_target="Cholesky" | custom-call | tf_op jit(solution)/shard_map/jit(cholesky)/cholesky | solution.py:48
  125.8 0.7 compare_reduce_fusion.1
  126.5 0.7 fusion.51
  127.2 2.4 %custom-call.6 = f32[1,32,32]{1,2,0:T(8,128)S(1)} custom-call(f32[1,32,32]{2,1,0:T(8,128)S(1)} %fusion.51), custom_call_target="InvertDiagBlocksLowerTriangular" | custom-call | tf_op jit(solution)/shard_map/triangular_solve/custom-call.0 | solution.py:49
  129.7 0.3 fusion.48
  130.0 7.4 %all-gather.5 = bf16[4,320,32]{1,2,0:T(8,128)(2,1)S(1)} all-gather(bf16[1,320,32]{1,2,0:T(8,128)(2,1)S(1)} %fusion.48), channel_id=1, replica_groups=mesh['row'=4,'col'=8] {'row'}, dimensions={0}, use_global_device_ids=true | all-gather | bytes 102400 | tf_op jit(solution)/shard_map/all_gather | solution.py:64
  137.4 0.2 copy.44
  137.7 4.9 %while.32 = (s32[]{:T(128)}, f32[5,512,32]{1,2,0:T(8,128)S(1)}, f32[5,512]{1,0:T(8,128)S(1)}, f32[1280]{0:T(1024)S(1)}, bf16[5,512,64]{2,1,0:T(8,128)(2,1)S(1)},...) while((s32[]{:T(128)}, f32[5,512,32]{1,2,0:T(8,128)S(1)}, ...), condition=%wide.region_13.16_spmd, body=%wide.region_12.15_spmd.sunk | while | flops 129105920 | bytes 867417 | solution.py:38
  137.7 1.0 fusion.85
  138.7 1.0 fusion.85
  139.6 1.0 fusion.85
  140.6 1.0 fusion.85
  141.6 1.0 fusion.85
  142.6 1.5 copy.54
  144.1 31.5 %reduce-scatter.9.cloned.1.call-done = f32[320,32]{1,0:T(8,128)} async-done(((f32[2560,32]{1,0:T(8,128)}), f32[320,32]{1,0:T(8,128)}) %reduce-scatter.9.cloned.1.call-update) | async-done | bytes 40976
  175.6 1.0 copy.48
  176.6 0.2 fusion.50
  176.8 40.0 %all-gather.1 = f32[1024,32]{1,0:T(8,128)S(1)} all-gather(f32[32,32]{1,0:T(8,128)S(1)} %fusion.50), channel_id=3, replica_groups=mesh['row'=4,'col'=8] {'row','col'}, dimensions={0}, use_global_device_ids=true | all-gather | bytes 135168 | tf_op jit(solution)/shard_map/all_gather | solution.py:47
  217.0 2.9 %cholesky.55 = f32[32,32]{1,0:T(8,128)S(1)} custom-call(f32[32,32]{1,0:T(8,128)S(1)} %fusion.54), custom_call_target="Cholesky" | custom-call | tf_op jit(solution)/shard_map/jit(cholesky)/cholesky | solution.py:48
  219.9 0.6 compare_reduce_fusion
  220.6 0.7 fusion.52
  221.2 2.4 %custom-call.7 = f32[1,32,32]{1,2,0:T(8,128)S(1)} custom-call(f32[1,32,32]{2,1,0:T(8,128)S(1)} %fusion.52), custom_call_target="InvertDiagBlocksLowerTriangular" | custom-call | tf_op jit(solution)/shard_map/triangular_solve/custom-call.0 | solution.py:49
  223.7 0.9 convolution_bitcast_fusion
  (50 shorter events, 1.7 us)
Async XLA Ops:
  6.5 74.9 %reduce-scatter.7.cloned.1.call-start = ((), (), s32[]{:S(2)}) async-start(), calls=%async_computation.2 | async-start | bytes 1474560
  32.1 1.0 copy-start
  47.8 127.8 %reduce-scatter.9.cloned.1.call-start = ((), (), s32[]{:S(2)}) async-start(), calls=%async_computation.3 | async-start | bytes 1474560
  47.9 4.8 %copy-start.1 = (u32[32]{0:T(128)S(1)}, u32[32]{0:T(128)}, u32[]{:S(2)}) copy-start(u32[32]{0:T(128)} %constant.83) | copy-start | bytes 388
Sparse Core Ops, SparseCore 0:
  47.9 33.4 reduce-scatter.6
  144.2 31.3 reduce-scatter.8
